TPU v7x, 32 devices: a whole 2x2x4 slice. The times are simulated.
32 devices in a mesh: gy: 8 (over y, x, core), gz: 4 (over z).
Axes of the slice: x: 2, y: 2, z: 4, core: 2. Of those that a mesh axis runs over, the one named last changes fastest.
Arguments:
- observed: float32 [512, 128, 128], P(None, 'gy', 'gz'), may hold values from -6 to 6
- bregman: float32 [3, 512, 128, 128], P(None, None, 'gy', 'gz'), may hold values from -6 to 6
Outputs:
- solution: float32 [512, 128, 128], P(None, 'gy', 'gz')
- bregman_out: float32 [3, 512, 128, 128], P(None, None, 'gy', 'gz')
All inputs are finite; a program needn't handle non-finite values.
Results may differ from a plain program's by a relative error of at most 0.0003.
Values sent between devices are 32-bit elements.
A program may use at most 128 MiB of HBM per device.

v0:
```python
import jax
import jax.numpy as jnp
from jax import lax
from jax.sharding import PartitionSpec as P

ITERS = 3


fidelity = 1.0
penalty = 2.0
threshold = 0.5


def shifted(value, axis, by):
    size = lax.axis_size(axis)
    pairs = [(i, i + by) for i in range(size) if 0 <= i + by < size]
    return lax.ppermute(value, axis, pairs)


def cosine_matrix(length):
    wave = lax.broadcasted_iota(jnp.int32, (length, length), 0)
    sample = lax.broadcasted_iota(jnp.int32, (length, length), 1)
    phase = (2 * sample + 1) * wave % (4 * length)
    factor = jnp.where(wave == 0, jnp.sqrt(1.0 / length), jnp.sqrt(2.0 / length)).astype(
        jnp.float32
    )
    return factor * jnp.cos(jnp.pi * phase.astype(jnp.float32) / (2.0 * length))


def transform(volume, matrix, position):
    patterns = ("kn,nbc->kbc", "kn,anc->akc", "kn,abn->abk")
    return jnp.einsum(patterns[position], matrix, volume, precision=lax.Precision.HIGHEST)


def laplace_values(start, width, length):
    wave = start + lax.iota(jnp.int32, width)
    return 2.0 - 2.0 * jnp.cos(jnp.pi * wave.astype(jnp.float32) / length)


def solve(source):
    extent_x = source.shape[0]
    full_y = source.shape[1] * lax.axis_size("gy")
    full_z = source.shape[2] * lax.axis_size("gz")
    matrix_x = cosine_matrix(extent_x)
    matrix_y = cosine_matrix(full_y)
    matrix_z = cosine_matrix(full_z)
    spectra = transform(source, matrix_x, 0)
    spectra = lax.all_to_all(spectra, "gz", split_axis=0, concat_axis=2, tiled=True)
    spectra = transform(spectra, matrix_z, 2)
    spectra = lax.all_to_all(spectra, "gy", split_axis=0, concat_axis=1, tiled=True)
    spectra = transform(spectra, matrix_y, 1)
    block_x = spectra.shape[0]
    start_x = (lax.axis_index("gz") * lax.axis_size("gy") + lax.axis_index("gy")) * block_x
    values_x = laplace_values(start_x, block_x, extent_x)
    values_y = laplace_values(0, full_y, full_y)
    values_z = laplace_values(0, full_z, full_z)
    divisor = fidelity + penalty * (
        values_x[:, None, None] + values_y[None, :, None] + values_z[None, None, :]
    )
    spectra = spectra / divisor
    spectra = transform(spectra, matrix_y.T, 1)
    spectra = lax.all_to_all(spectra, "gy", split_axis=1, concat_axis=0, tiled=True)
    spectra = transform(spectra, matrix_z.T, 2)
    spectra = lax.all_to_all(spectra, "gz", split_axis=2, concat_axis=0, tiled=True)
    return transform(spectra, matrix_x.T, 0)


def shrink(values):
    return jnp.sign(values) * jnp.maximum(jnp.abs(values) - threshold, 0.0)


def gradients(volume, keep_y, keep_z):
    next_y = shifted(volume[:, :1, :], "gy", -1)
    next_z = shifted(volume[:, :, :1], "gz", -1)
    slope_x = jnp.concatenate([volume[1:] - volume[:-1], jnp.zeros_like(volume[:1])], axis=0)
    slope_y = jnp.where(keep_y, jnp.concatenate([volume[:, 1:, :], next_y], axis=1) - volume, 0.0)
    slope_z = jnp.where(keep_z, jnp.concatenate([volume[:, :, 1:], next_z], axis=2) - volume, 0.0)
    return jnp.stack([slope_x, slope_y, slope_z])


def adjoint(fluxes, lower_y, lower_z):
    result = jnp.concatenate([jnp.zeros_like(fluxes[0][:1]), fluxes[0][:-1]], axis=0) - fluxes[0]
    result = result + (jnp.concatenate([lower_y, fluxes[1][:, :-1, :]], axis=1) - fluxes[1])
    return result + (jnp.concatenate([lower_z, fluxes[2][:, :, :-1]], axis=2) - fluxes[2])


def per_device(observed, bregman):
    extent_x, cells_y, cells_z = observed.shape
    index_y = lax.broadcasted_iota(jnp.int32, (1, cells_y, 1), 1) + lax.axis_index("gy") * cells_y
    index_z = lax.broadcasted_iota(jnp.int32, (1, 1, cells_z), 2) + lax.axis_index("gz") * cells_z
    keep_y = index_y < cells_y * lax.axis_size("gy") - 1
    keep_z = index_z < cells_z * lax.axis_size("gz") - 1
    keep_x = lax.broadcasted_iota(jnp.int32, (extent_x, 1, 1), 0) < extent_x - 1
    slopes = gradients(observed, keep_y, keep_z)
    shrunk = shrink(slopes + bregman)
    solution = observed
    for iteration in range(ITERS):
        excess = shrunk - bregman
        fluxes = jnp.stack(
            [
                jnp.where(keep_x, excess[0], 0.0),
                jnp.where(keep_y, excess[1], 0.0),
                jnp.where(keep_z, excess[2], 0.0),
            ]
        )
        lower_y = shifted(fluxes[1][:, -1:, :], "gy", 1)
        lower_z = shifted(fluxes[2][:, :, -1:], "gz", 1)
        source = fidelity * observed + penalty * adjoint(fluxes, lower_y, lower_z)
        solution = solve(source)
        slopes = gradients(solution, keep_y, keep_z)
        shrunk = shrink(slopes + bregman)
        bregman = bregman + slopes - shrunk
    return (solution, bregman)


def solution(mesh):
    return jax.shard_map(
        per_device,
        mesh=mesh,
        in_specs=(P(None, "gy", "gz"), P(None, None, "gy", "gz")),
        out_specs=(P(None, "gy", "gz"), P(None, None, "gy", "gz")),
        check_vma=False,
    )
```

profile of v0, /device:TPU:0, one launch (start us, length us, event | category | flops | bytes accessed | tf_op | source)
XLA Modules:
  0.0 497.8 jit_solution(7941197379964932244)
XLA Ops:
  5.1 3.0 slice_subtract_fusion.3
  13.4 5.6 %collective-permute-start.3 = (f32[512,16,1]{0,2,1:T(1,128)S(1)}, f32[512,16,1]{0,2,1:T(1,128)S(1)}, u32[]{:S(2)}, u32[]{:S(2)}) collective-permute-start(f32[512,16,1]{0,2,1:T(1,128)S(1)} %slice.198), channel_id=1, source_target_pairs={{0,1},{1,2},{2,3},{4,5},{5,6},{6,7},{8,9},{9,10},{10,11},{12,13},{... | collective-permute-start | bytes 98312 | tf_op jit(solution)/shard_map/ppermute | solution.py:17
  19.0 2.8 collective-permute-start.2
  23.6 5.8 %fusion.68 = f32[512,512]{0,1:S(1)} fusion(f32[512,512]{0,1:T(8,128)S(1)} %bitcast.240, s32[512]{0:T(512)S(1)} %multiply_add_fusion.1, f32[512]{0:T(512)S(1)} %fusion.169), kind=kOutput, calls=%fused_computation.112 | convolution fusion | flops 1614544896 | bytes 2101248
  29.4 3.7 copy.64
  33.0 4.8 reshape.96
  37.9 4.5 all-to-all-start
  42.4 26.3 %all-to-all-done = f32[4,1,65536]{2,1,0:T(1,128)S(1)} async-done(((f32[4,1,65536]{2,1,0:T(1,128)}), f32[4,1,65536]{2,1,0:T(1,128)S(1)}, u32[]{:S(2)}, u32[]{:S(2)}) %all-to-all-start) | async-done | bytes 1048608 | tf_op jit(solution)/shard_map/all_to_all | solution.py:48
  69.3 3.7 reduce
  73.0 3.4 reshape.97
  76.4 2.8 copy.112
  82.1 4.7 all-to-all-start.1
  87.0 15.4 %all-to-all-done.1 = f32[128,16,128]{2,1,0:T(8,128)S(1)} async-done(((f32[128,16,128]{2,1,0:T(8,128)}), f32[128,16,128]{2,1,0:T(8,128)S(1)}, u32[]{:S(2)}, u32[]{:S(2)}) %all-to-all-start.1) | async-done | bytes 1048608 | tf_op jit(solution)/shard_map/all_to_all | solution.py:50
  106.3 18.2 %all_to_all.216 = f32[16,128,128]{2,0,1:T(8,128)S(1)} all-to-all(f32[16,128,128]{2,0,1:T(8,128)S(1)} %copy.71), channel_id=1, replica_groups=mesh['gy'=8,'gz'=4] {'gy'}, dimensions={1} | all-to-all | bytes 2097152 | tf_op jit(solution)/shard_map/all_to_all | solution.py:62
  126.4 29.4 %all_to_all.217 = f32[128,16,128]{0,1,2:T(8,128)S(1)} all-to-all(f32[128,16,128]{0,1,2:T(8,128)S(1)} %copy.74), channel_id=1, replica_groups=mesh['gy'=8,'gz'=4] {'gz'}, dimensions={2} | all-to-all | bytes 2097152 | tf_op jit(solution)/shard_map/all_to_all | solution.py:64
  156.5 5.8 %fusion.18 = f32[512,512]{0,1:S(1)} fusion(f32[64,8,4,128]{3,2,1,0:T(4,128)S(1)} %bitcast.237, s32[512]{0:T(512)S(1)} %multiply_add_fusion.1, f32[512]{0:T(512)S(1)} %fusion.169), kind=kOutput, calls=%fused_computation.35 | convolution fusion | flops 1614544896 | bytes 2101248
  165.7 2.9 collective-permute-done.5
  172.9 4.3 collective-permute-start.7
  179.6 6.8 %fusion.65 = f32[512,512]{0,1} fusion(f32[512,512]{0,1:T(8,128)S(1)} %bitcast.241, s32[512]{0:T(512)S(1)} %multiply_add_fusion.1, f32[512]{0:T(512)S(1)} %fusion.169), kind=kOutput, calls=%fused_computation.111 | convolution fusion | flops 1614544896 | bytes 2101248
  186.4 4.6 copy.77
  191.0 4.8 reshape.98
  195.8 29.8 %all_to_all.218 = f32[4,1,65536]{2,1,0:T(1,128)} all-to-all(f32[4,1,65536]{2,1,0:T(1,128)} %reshape.98), channel_id=1, replica_groups=mesh['gy'=8,'gz'=4] {'gz'}, dimensions={0} | all-to-all | bytes 2097152 | tf_op jit(solution)/shard_map/all_to_all | solution.py:48
  225.6 5.6 %reduce.1 = f32[4,65536]{1,0:T(4,128)} reduce(f32[4,1,65536]{2,1,0:T(1,128)} %all_to_all.218, f32[]{:T(128)} %broadcast.306), dimensions={1}, to_apply=%all_to_all.172.reduce_sub_computation | reduce | bytes 2097156 | tf_op jit(solution)/shard_map/all_to_all | solution.py:48
  231.2 4.6 reshape.99
  235.8 3.6 copy.116
  241.7 2.6 copy.106
  246.8 18.1 %all_to_all.219 = f32[128,16,128]{2,1,0:T(8,128)S(1)} all-to-all(f32[128,16,128]{2,1,0:T(8,128)S(1)} %fusion.89), channel_id=1, replica_groups=mesh['gy'=8,'gz'=4] {'gy'}, dimensions={0} | all-to-all | bytes 2097152 | tf_op jit(solution)/shard_map/all_to_all | solution.py:50
  269.3 2.6 copy.84
  272.0 19.2 %all_to_all.220 = f32[16,128,128]{2,0,1:T(8,128)S(1)} all-to-all(f32[16,128,128]{2,0,1:T(8,128)} %copy.84), channel_id=1, replica_groups=mesh['gy'=8,'gz'=4] {'gy'}, dimensions={1} | all-to-all | bytes 2097152 | tf_op jit(solution)/shard_map/all_to_all | solution.py:62
  293.5 2.6 copy.87
  296.1 28.9 %all_to_all.221 = f32[128,16,128]{0,1,2:T(8,128)S(1)} all-to-all(f32[128,16,128]{0,1,2:T(8,128)} %copy.87), channel_id=1, replica_groups=mesh['gy'=8,'gz'=4] {'gz'}, dimensions={2} | all-to-all | bytes 2097152 | tf_op jit(solution)/shard_map/all_to_all | solution.py:64
  325.7 5.8 %fusion.15 = f32[512,512]{0,1:S(1)} fusion(f32[64,8,4,128]{3,2,1,0:T(4,128)S(1)} %bitcast.239, s32[512]{0:T(512)S(1)} %multiply_add_fusion.1, f32[512]{0:T(512)S(1)} %fusion.169), kind=kOutput, calls=%fused_computation.32 | convolution fusion | flops 1614544896 | bytes 2101248
  334.9 2.8 collective-permute-done.9
  338.4 3.9 fusion
  342.7 4.4 collective-permute-start.10
  347.2 4.7 collective-permute-start.11
  354.3 5.8 %fusion.62 = f32[512,512]{0,1:S(1)} fusion(f32[512,512]{0,1:T(8,128)S(1)} %bitcast.242, s32[512]{0:T(512)S(1)} %multiply_add_fusion.1, f32[512]{0:T(512)S(1)} %fusion.169), kind=kOutput, calls=%fused_computation.110 | convolution fusion | flops 1614544896 | bytes 2101248
  360.0 3.7 copy.90
  363.7 3.9 reshape.100
  367.6 28.3 %all_to_all.222 = f32[4,1,65536]{2,1,0:T(1,128)S(1)} all-to-all(f32[4,1,65536]{2,1,0:T(1,128)S(1)} %reshape.100), channel_id=1, replica_groups=mesh['gy'=8,'gz'=4] {'gz'}, dimensions={0} | all-to-all | bytes 2097152 | tf_op jit(solution)/shard_map/all_to_all | solution.py:48
  395.9 3.7 reduce.2
  399.6 3.4 reshape.101
  403.0 2.8 copy.120
  407.8 18.7 %all_to_all.223 = f32[128,16,128]{2,1,0:T(8,128)S(1)} all-to-all(f32[128,16,128]{2,1,0:T(8,128)S(1)} %fusion.83), channel_id=1, replica_groups=mesh['gy'=8,'gz'=4] {'gy'}, dimensions={0} | all-to-all | bytes 2097152 | tf_op jit(solution)/shard_map/all_to_all | solution.py:50
  430.4 18.0 %all_to_all.224 = f32[16,128,128]{2,0,1:T(8,128)S(1)} all-to-all(f32[16,128,128]{2,0,1:T(8,128)S(1)} %copy.97), channel_id=1, replica_groups=mesh['gy'=8,'gz'=4] {'gy'}, dimensions={1} | all-to-all | bytes 2097152 | tf_op jit(solution)/shard_map/all_to_all | solution.py:62
  450.3 29.5 %all_to_all.225 = f32[128,16,128]{0,1,2:T(8,128)S(1)} all-to-all(f32[128,16,128]{0,1,2:T(8,128)S(1)} %copy.100), channel_id=1, replica_groups=mesh['gy'=8,'gz'=4] {'gz'}, dimensions={2} | all-to-all | bytes 2097152 | tf_op jit(solution)/shard_map/all_to_all | solution.py:64
  480.5 5.8 %fusion.12 = f32[512,512]{0,1:S(1)} fusion(f32[64,8,4,128]{3,2,1,0:T(4,128)S(1)} %bitcast.235, s32[512]{0:T(512)S(1)} %multiply_add_fusion.1, f32[512]{0:T(512)S(1)} %fusion.169), kind=kOutput, calls=%fused_computation.29 | convolution fusion | flops 1614544896 | bytes 2101248
  493.1 4.2 multiply_subtract_fusion
  (123 shorter events, 65.1 us)
Async XLA Ops:
  1.6 8.1 %collective-permute-start.1 = (f32[512,16,1]{0,2,1:T(1,128)S(1)}, f32[512,16,1]{0,2,1:T(1,128)S(1)}, u32[]{:S(2)}, u32[]{:S(2)}) collective-permute-start(f32[512,16,1]{0,2,1:T(1,128)S(1)} %slice.149), channel_id=1, source_target_pairs={{1,0},{2,1},{3,2},{5,4},{6,5},{7,6},{9,8},{10,9},{11,10},{13,12},{... | collective-permute-start | bytes 98312 | tf_op jit(solution)/shard_map/ppermute | solution.py:17
  3.8 6.0 %collective-permute-start = (f32[512,1,32]{0,2,1:T(8,128)S(1)}, f32[512,1,32]{0,2,1:T(8,128)S(1)}, u32[]{:S(2)}, u32[]{:S(2)}) collective-permute-start(f32[512,1,32]{0,2,1:T(8,128)S(1)} %slice.147), channel_id=1, source_target_pairs={{4,0},{8,4},{12,8},{16,12},{20,16},{24,20},{28,24},{5,1},{9,5},{13... | collective-permute-start | bytes 196616 | tf_op jit(solution)/shard_map/ppermute | solution.py:17
  5.1 4.5 copy-start
  8.1 1.6 slice-start
  9.7 1.9 copy-start.1
  13.4 8.5 %collective-permute-start.3 = (f32[512,16,1]{0,2,1:T(1,128)S(1)}, f32[512,16,1]{0,2,1:T(1,128)S(1)}, u32[]{:S(2)}, u32[]{:S(2)}) collective-permute-start(f32[512,16,1]{0,2,1:T(1,128)S(1)} %slice.198), channel_id=1, source_target_pairs={{0,1},{1,2},{2,3},{4,5},{5,6},{6,7},{8,9},{9,10},{10,11},{12,13},{... | collective-permute-start | bytes 98312 | tf_op jit(solution)/shard_map/ppermute | solution.py:17
  19.0 3.6 collective-permute-start.2
  37.9 30.9 %all-to-all-start = ((f32[4,1,65536]{2,1,0:T(1,128)}), f32[4,1,65536]{2,1,0:T(1,128)S(1)}, u32[]{:S(2)}, u32[]{:S(2)}) async-start(f32[4,1,65536]{2,1,0:T(1,128)} %reshape.96), calls=%async_computation | async-start | bytes 2097152 | tf_op jit(solution)/shard_map/all_to_all | solution.py:48
  82.1 20.3 %all-to-all-start.1 = ((f32[128,16,128]{2,1,0:T(8,128)}), f32[128,16,128]{2,1,0:T(8,128)S(1)}, u32[]{:S(2)}, u32[]{:S(2)}) async-start(f32[128,16,128]{2,1,0:T(8,128)} %fusion.95), calls=%async_computation.1 | async-start | bytes 2097152 | tf_op jit(solution)/shard_map/all_to_all | solution.py:50
  162.7 5.8 %collective-permute-start.5 = (f32[512,16,1]{0,2,1:T(1,128)S(1)}, f32[512,16,1]{0,2,1:T(1,128)S(1)}, u32[]{:S(2)}, u32[]{:S(2)}) collective-permute-start(f32[512,16,1]{0,2,1:T(1,128)S(1)} %slice.205), channel_id=1, source_target_pairs={{1,0},{2,1},{3,2},{5,4},{6,5},{7,6},{9,8},{10,9},{11,10},{13,12},{... | collective-permute-start | bytes 98312 | tf_op jit(solution)/shard_map/ppermute | solution.py:17
  164.0 4.5 collective-permute-start.4
  165.6 3.4 copy-start.2
  169.1 1.5 copy-start.6
  171.0 7.7 %collective-permute-start.6 = (f32[512,1,32]{0,2,1:T(8,128)S(1)}, f32[512,1,32]{0,2,1:T(8,128)S(1)}, u32[]{:S(2)}, u32[]{:S(2)}) collective-permute-start(f32[512,1,32]{0,2,1:T(8,128)S(1)} %slice.209), channel_id=1, source_target_pairs={{0,4},{4,8},{8,12},{12,16},{16,20},{20,24},{24,28},{1,5},{5,9},{9,... | collective-permute-start | bytes 196616 | tf_op jit(solution)/shard_map/ppermute | solution.py:17
  172.9 5.7 %collective-permute-start.7 = (f32[512,16,1]{0,2,1:T(1,128)S(1)}, f32[512,16,1]{0,2,1:T(1,128)S(1)}, u32[]{:S(2)}, u32[]{:S(2)}) collective-permute-start(f32[512,16,1]{0,2,1:T(1,128)S(1)} %slice.212), channel_id=1, source_target_pairs={{0,1},{1,2},{2,3},{4,5},{5,6},{6,7},{8,9},{9,10},{10,11},{12,13},{... | collective-permute-start | bytes 98312 | tf_op jit(solution)/shard_map/ppermute | solution.py:17
  332.0 5.8 %collective-permute-start.9 = (f32[512,16,1]{0,2,1:T(1,128)S(1)}, f32[512,16,1]{0,2,1:T(1,128)S(1)}, u32[]{:S(2)}, u32[]{:S(2)}) collective-permute-start(f32[512,16,1]{0,2,1:T(1,128)S(1)} %slice.219), channel_id=1, source_target_pairs={{1,0},{2,1},{3,2},{5,4},{6,5},{7,6},{9,8},{10,9},{11,10},{13,12},{... | collective-permute-start | bytes 98312 | tf_op jit(solution)/shard_map/ppermute | solution.py:17
  333.3 4.5 collective-permute-start.8
  334.9 3.4 copy-start.3
  334.9 3.4 copy-start.7
  342.7 10.6 %collective-permute-start.10 = (f32[512,1,32]{0,2,1:T(8,128)S(1)}, f32[512,1,32]{0,2,1:T(8,128)S(1)}, u32[]{:S(2)}, u32[]{:S(2)}) collective-permute-start(f32[512,1,32]{0,2,1:T(8,128)S(1)} %slice.223), channel_id=1, source_target_pairs={{0,4},{4,8},{8,12},{12,16},{16,20},{20,24},{24,28},{1,5},{5,9},{9,... | collective-permute-start | bytes 196616 | tf_op jit(solution)/shard_map/ppermute | solution.py:17
  347.2 6.1 %collective-permute-start.11 = (f32[512,16,1]{0,2,1:T(1,128)S(1)}, f32[512,16,1]{0,2,1:T(1,128)S(1)}, u32[]{:S(2)}, u32[]{:S(2)}) collective-permute-start(f32[512,16,1]{0,2,1:T(1,128)S(1)} %slice.226), channel_id=1, source_target_pairs={{0,1},{1,2},{2,3},{4,5},{5,6},{6,7},{8,9},{9,10},{10,11},{12,13},{... | collective-permute-start | bytes 98312 | tf_op jit(solution)/shard_map/ppermute | solution.py:17
  486.3 6.2 %copy-start.4 = (f32[512,512]{0,1}, f32[512,512]{0,1:S(1)}, u32[]{:S(2)}) copy-start(f32[512,512]{0,1:S(1)} %fusion.12) | copy-start | bytes 3145732
  486.7 5.8 %collective-permute-start.13 = (f32[512,16,1]{0,2,1:T(1,128)S(1)}, f32[512,16,1]{0,2,1:T(1,128)S(1)}, u32[]{:S(2)}, u32[]{:S(2)}) collective-permute-start(f32[512,16,1]{0,2,1:T(1,128)S(1)} %slice.233), channel_id=1, source_target_pairs={{1,0},{2,1},{3,2},{5,4},{6,5},{7,6},{9,8},{10,9},{11,10},{13,12},{... | collective-permute-start | bytes 98312 | tf_op jit(solution)/shard_map/ppermute | solution.py:17
  488.0 4.5 collective-permute-start.12
  490.0 3.1 copy-start.5
where the time goes:
time: 508 us; the launch traced here: 498 us
  blocking collectives  238 us (47%)
  local copies, waits for them, and re-layouts  69.1 us (14%)
  matrix products  57.2 us (11%)
  waiting for transfers between devices  53.4 us (11%)
  starting transfers between devices  43.5 us (9%)
  other arithmetic  34.3 us (7%)
    all_to_all x3, blocking collectives, solve(): lax.all_to_all(spectra, 'gz', split_axis=2, concat_axis=0, tiled=True)  87.8 us
    all_to_all x2, blocking collectives, solve(): lax.all_to_all(spectra, 'gz', split_axis=0, concat_axis=2, tiled=True)  58.1 us
    all_to_all x3, blocking collectives, solve(): lax.all_to_all(spectra, 'gy', split_axis=1, concat_axis=0, tiled=True)  55.5 us
    all_to_all x2, blocking collectives, solve(): lax.all_to_all(spectra, 'gy', split_axis=0, concat_axis=1, tiled=True)  36.8 us
    unnamed x6, matrix products  35.8 us
    ppermute x14, starting transfers between devices, shifted(): return lax.ppermute(value, axis, pairs)  34.3 us
    unnamed x22, local copies, waits for them, and re-layouts  26.4 us
    all_to_all x1, waiting for transfers between devices, solve(): lax.all_to_all(spectra, 'gz', split_axis=0, concat_axis=2, tiled=True)  26.3 us
  transfers between devices with their start and end apart: 16, of which 8 were waited for; matrix products, arithmetic and copies ran while one was open for 1% of the time, Pallas kernels for 0%

commit v1 on v0

v1 whole, which is shorter than its diff:
```python
import functools

import jax
import jax.numpy as jnp
import numpy as np
from jax import lax
from jax.experimental import pallas as pl
from jax.experimental.pallas import tpu as pltpu
from jax.sharding import PartitionSpec as P

ITERS = 3
fidelity = 1.0
penalty = 2.0
threshold = 0.5
LANES = 128
OCTET = 8


def cosine_matrix(length):
    wave = np.arange(length)[:, None]
    sample = np.arange(length)[None, :]
    factor = np.where(wave == 0, np.sqrt(1.0 / length), np.sqrt(2.0 / length))
    return factor * np.cos(np.pi * ((2 * sample + 1) * wave % (4 * length)) / (2.0 * length))


def laplace_values(length):
    return 4.0 * np.sin(np.pi * np.arange(length) / (2.0 * length)) ** 2


def halves(matrix):
    matrix = matrix.astype(np.float32)
    high = matrix.astype(jnp.bfloat16)
    low = (matrix - high.astype(np.float32)).astype(jnp.bfloat16)
    return high, low


def split(values):
    high = values.astype(jnp.bfloat16)
    return high, (values - high.astype(jnp.float32)).astype(jnp.bfloat16)


def product(left, right, dims):
    dot = functools.partial(
        lax.dot_general, dimension_numbers=(dims, ((), ())), preferred_element_type=jnp.float32
    )
    return dot(left[0], right[0]) + (dot(left[0], right[1]) + dot(left[1], right[0]))


def swap_groups(arrays):
    arrays = list(arrays)
    lane = lax.broadcasted_iota(jnp.int32, arrays[0].shape, 1)
    for bit in (1, 2, 4):
        upper = (lane & bit) != 0
        for low in range(OCTET):
            if low & bit:
                continue
            first, second = arrays[low], arrays[low | bit]
            arrays[low] = jnp.where(upper, pltpu.roll(second, bit, 1), first)
            arrays[low | bit] = jnp.where(upper, second, pltpu.roll(first, LANES - bit, 1))
    return arrays


def clip(values):
    return jnp.minimum(jnp.maximum(values, -threshold), threshold)


def kernel(
    size_y, size_z,
    f_ref, b_in, xh, xl, yh, yl, th, tl, ex_ref, ey_ref,
    u_ref, b_ref,
    src, spec, front, depth, gain, tail, back, arrive, home, ends, gathered, chain, edge,
    next_y, last_y, next_z, last_z, pack_z, low_by, low_bz,
    fs, fr, bs, br, zs, zr, hs, hr,
):
    iy, iz = lax.axis_index("gy"), lax.axis_index("gz")
    cells_y, cells_z, extent = f_ref.shape
    octets = cells_z // OCTET
    part = extent // size_y
    groups = size_y // OCTET
    rows = cells_y * OCTET

    def at_y(d):
        return lax.rem(iy + d, size_y)

    def at_z(d):
        return lax.rem(iz + d, size_z)

    barrier = pltpu.get_barrier_semaphore()
    for d in range(1, size_y):
        pl.semaphore_signal(barrier, inc=1, device_id={"gy": at_y(d)}, device_id_type=pl.DeviceIdType.MESH)
    for d in range(1, size_z):
        pl.semaphore_signal(barrier, inc=1, device_id={"gz": at_z(d)}, device_id_type=pl.DeviceIdType.MESH)
    pl.semaphore_wait(barrier, size_y + size_z - 2)

    def remote(source, target, send, recv, device):
        return pltpu.make_async_remote_copy(
            src_ref=source, dst_ref=target, send_sem=send, recv_sem=recv,
            device_id=device, device_id_type=pl.DeviceIdType.MESH,
        )

    def halo_start(volume, slot):
        pack_z[slot, 0] = volume[:, 0, :]
        pack_z[slot, 1] = volume[:, cells_z - 1, :]
        copies = [
            remote(volume.at[0], next_y.at[slot], hs.at[slot, 0], hr.at[slot, 0], {"gy": at_y(size_y - 1)}),
            remote(volume.at[cells_y - 1], last_y.at[slot], hs.at[slot, 1], hr.at[slot, 1], {"gy": at_y(1)}),
            remote(pack_z.at[slot, 0], next_z.at[slot], hs.at[slot, 2], hr.at[slot, 2], {"gz": at_z(size_z - 1)}),
            remote(pack_z.at[slot, 1], last_z.at[slot], hs.at[slot, 3], hr.at[slot, 3], {"gz": at_z(1)}),
        ]
        for copy in copies:
            copy.start()
        return copies

    edge[...] = b_in[2, :, cells_z - 1, :]
    copies = halo_start(f_ref, 0)
    extra = [
        remote(b_in.at[1, cells_y - 1], low_by, hs.at[0, 4], hr.at[0, 4], {"gy": at_y(1)}),
        remote(edge, low_bz, hs.at[0, 5], hr.at[0, 5], {"gz": at_z(1)}),
    ]
    for copy in extra:
        copy.start()

    centre = (
        fidelity / penalty + 2.0
        + jnp.concatenate([ex_ref[pl.ds(pl.multiple_of(iy * part, part), part), :]] * groups, axis=1)
        + ey_ref[0:1, :]
    )

    def eliminate(first, final, keep):
        level = 1.0 / (centre - first)
        run = level
        corner = level
        if keep:
            gain[0] = level
            tail[0] = run

        def step(j, carry):
            level, run, corner = carry
            level = 1.0 / (centre - jnp.where(j == cells_z - 1, final, 0.0) - level)
            after = run * level
            corner = corner + run * after
            if keep:
                gain[j] = level
                tail[j] = after
            return level, after, corner

        return lax.fori_loop(1, cells_z, step, (level, run, corner))

    own_end, own_far, own_start = eliminate(
        jnp.where(iz == 0, 1.0, 0.0), jnp.where(iz == size_z - 1, 1.0, 0.0), True
    )
    mid_end, mid_far, mid_start = eliminate(0.0, 0.0, False)
    linked, _, _ = eliminate(1.0, 0.0, False)
    zero = jnp.zeros_like(centre)
    left_link = zero
    right_link = zero
    for q in range(size_z - 1):
        if q > 0:
            ratio = mid_far * linked / (1.0 - mid_start * linked)
            chain[q, 0] = mid_far + ratio * mid_start
            chain[q, 1] = ratio
            linked = mid_end + mid_far * ratio
        left_link = jnp.where(iz == q + 1, linked, left_link)
        right_link = jnp.where(size_z - 2 - iz == q, linked, right_link)
    one_l = 1.0 - own_start * left_link
    one_r = 1.0 - own_end * right_link
    cross_l = own_far * left_link
    cross_r = own_far * right_link
    scale = 1.0 / (one_l * one_r - cross_l * cross_r)
    home[0] = left_link
    home[1] = right_link
    home[2] = one_l * scale
    home[3] = one_r * scale
    home[4] = cross_l * scale
    home[5] = cross_r * scale
    home[6] = own_start
    home[7] = own_end
    home[8] = own_far

    for copy in copies + extra:
        copy.wait()

    lane_x = lax.broadcasted_iota(jnp.int32, (cells_z, extent), 1)
    row_z = lax.broadcasted_iota(jnp.int32, (cells_z, extent), 0)
    keep_x = lane_x < extent - 1
    keep_z = jnp.logical_or(row_z < cells_z - 1, iz < size_z - 1)

    def pointwise(volume, slopes_b, slot, first):
        def flux(slope, old):
            total = slope + old
            new = clip(total)
            return new, total - new - (old if first else new)

        new, lower_y = flux(volume[0] - last_y[slot], low_by[...])
        if not first:
            low_by[...] = new
        lower_y = jnp.where(iy > 0, lower_y, 0.0)
        new, lower_z = flux(pack_z[slot, 0] - last_z[slot], low_bz[...])
        if not first:
            low_bz[...] = new
        edge[...] = jnp.where(iz > 0, lower_z, 0.0)

        def plane(y, above, before, keep_y):
            value = volume[y]
            new, flux_x = flux(
                jnp.where(keep_x, pltpu.roll(value, extent - 1, 1) - value, 0.0), slopes_b[0, y]
            )
            b_ref[0, y] = slopes_b[0, y] if first else new
            flux_x = jnp.where(keep_x, flux_x, 0.0)
            new, flux_y = flux(jnp.where(keep_y, above - value, 0.0), slopes_b[1, y])
            b_ref[1, y] = slopes_b[1, y] if first else new
            flux_y = jnp.where(keep_y, flux_y, 0.0)
            beside = jnp.where(
                row_z < cells_z - 1, pltpu.roll(value, cells_z - 1, 0), next_z[slot, pl.ds(y, 1), :]
            )
            new, flux_z = flux(jnp.where(keep_z, beside - value, 0.0), slopes_b[2, y])
            b_ref[2, y] = slopes_b[2, y] if first else new
            flux_z = jnp.where(keep_z, flux_z, 0.0)
            under = jnp.where(row_z > 0, pltpu.roll(flux_z, 1, 0), edge[pl.ds(y, 1), :])
            src[y] = (
                (fidelity / penalty) * f_ref[y]
                + (pltpu.roll(flux_x, 1, 1) - flux_x)
                + (before - flux_y)
                + (under - flux_z)
            )
            return flux_y

        before = lax.fori_loop(
            0, cells_y - 1, lambda y, before: plane(y, volume[y + 1], before, True), lower_y
        )
        plane(cells_y - 1, next_y[slot], before, iy < size_y - 1)

    pointwise(f_ref, b_in, 0, True)

    def solve(slot):
        sent = []
        for o in range(octets):
            block = split(src[:, pl.ds(o * OCTET, OCTET), :].reshape(rows, extent))
            spec[o] = product((xh[...], xl[...]), block, ((1,), (1,)))
            for d in range(1, size_y):
                copy = remote(
                    spec.at[o, pl.ds(pl.multiple_of(at_y(d) * part, part), part)], front.at[o, iy],
                    fs.at[o, d], fr.at[o, d], {"gy": at_y(d)},
                )
                copy.start()
                sent.append(copy)
            front[o, iy] = spec[o, pl.ds(pl.multiple_of(iy * part, part), part), :]

        level = zero
        first = zero
        for o in range(octets):
            for copy in sent[o * (size_y - 1) : (o + 1) * (size_y - 1)]:
                copy.wait_recv()

            def regroup(r, _):
                at = pl.ds(pl.multiple_of(r * OCTET, OCTET), OCTET)
                for t in range(groups):
                    planes = swap_groups([front[o, t * OCTET + i, at, :] for i in range(OCTET)])
                    for i in range(OCTET):
                        depth[o * OCTET + i, at, pl.ds(t * LANES, LANES)] = planes[i]
                return 0

            lax.fori_loop(0, part // OCTET, regroup, 0, unroll=True)
            values = split(depth[pl.ds(o * OCTET, OCTET)].reshape(OCTET * part, size_y * cells_y))
            values = product(values, (yh[...], yl[...]), ((1,), (0,)))
            values = values.reshape(OCTET, part, size_y * cells_y)
            for i in range(OCTET):
                j = o * OCTET + i
                level = (values[i] + level) * gain[j]
                first = level if j == 0 else first + tail[j - 1] * level
                depth[j] = level
        ends[slot, 0] = first
        ends[slot, 1] = level
        gathered[slot, iz, 0] = first
        gathered[slot, iz, 1] = level

        around = []
        for d in range(1, size_z):
            copy = remote(
                ends.at[slot], gathered.at[slot, iz], zs.at[slot, d], zr.at[slot, d], {"gz": at_z(d)}
            )
            copy.start()
            around.append(copy)
        for copy in around:
            copy.wait_recv()
        left = zero
        right = zero
        for q in range(size_z - 1):
            here = gathered[slot, q, 1]
            there = gathered[slot, size_z - 1 - q, 0]
            if q > 0:
                here = here + chain[q, 0] * left + chain[q, 1] * gathered[slot, q, 0]
                there = there + chain[q, 0] * right + chain[q, 1] * gathered[slot, size_z - 1 - q, 1]
            left = jnp.where(q < iz, here, left)
            right = jnp.where(q < size_z - 1 - iz, there, right)
        bottom = first + home[6] * left + home[8] * right
        top = level + home[8] * left + home[7] * right
        from_left = left + home[0] * (home[3] * bottom + home[5] * top)
        value = right + home[1] * (home[2] * top + home[4] * bottom)

        returned = {}
        for o in reversed(range(octets)):
            for i in reversed(range(OCTET)):
                j = o * OCTET + i
                value = depth[j] + from_left * tail[j] + gain[j] * value
                depth[j] = value
            values = split(depth[pl.ds(o * OCTET, OCTET)].reshape(OCTET * part, size_y * cells_y))
            values = product(values, (th[...], tl[...]), ((1,), (0,)))
            depth[pl.ds(o * OCTET, OCTET)] = values.reshape(OCTET, part, size_y * cells_y)

            def ungroup(r, _):
                at = pl.ds(pl.multiple_of(r * OCTET, OCTET), OCTET)
                for t in range(groups):
                    planes = swap_groups(
                        [depth[o * OCTET + i, at, pl.ds(t * LANES, LANES)] for i in range(OCTET)]
                    )
                    for i in range(OCTET):
                        back[o, t * OCTET + i, at, :] = planes[i]
                return 0

            lax.fori_loop(0, part // OCTET, ungroup, 0, unroll=True)
            returned[o] = []
            for copy in sent[o * (size_y - 1) : (o + 1) * (size_y - 1)]:
                copy.wait_send()
            for d in range(1, size_y):
                copy = remote(
                    back.at[o, at_y(d)], arrive.at[o, pl.ds(pl.multiple_of(iy * part, part), part)],
                    bs.at[o, d], br.at[o, d], {"gy": at_y(d)},
                )
                copy.start()
                returned[o].append(copy)
            arrive[o, pl.ds(pl.multiple_of(iy * part, part), part), :] = back[o, iy]
        for o in reversed(range(octets)):
            for copy in returned[o]:
                copy.wait_recv()
            values = split(arrive[o].T)
            values = product(values, (xh[...], xl[...]), ((1,), (0,)))
            u_ref[:, pl.ds(o * OCTET, OCTET), :] = values.reshape(cells_y, OCTET, extent)
        for o in range(octets):
            for copy in returned[o]:
                copy.wait_send()
        for copy in around:
            copy.wait_send()

    def iteration(it, carry):
        solve(it)
        for copy in halo_start(u_ref, it + 1):
            copy.wait()
        pointwise(u_ref, b_ref, it + 1, False)
        return carry

    lax.fori_loop(0, ITERS, iteration, 0)


def per_device(size_y, size_z, observed, bregman):
    f = jnp.transpose(observed, (1, 2, 0))
    b = jnp.transpose(bregman, (0, 2, 3, 1))
    cells_y, cells_z, extent = f.shape
    full_y = cells_y * size_y
    part = extent // size_y
    octets = cells_z // OCTET
    groups = size_y // OCTET
    order = np.array(
        [
            (t * OCTET + i) * cells_y + y
            for t in range(groups)
            for y in range(cells_y)
            for i in range(OCTET)
        ]
    )
    matrix_y = cosine_matrix(full_y)[:, order]
    waves_x = np.broadcast_to(laplace_values(extent)[:, None], (extent, LANES))
    waves_y = np.broadcast_to(laplace_values(full_y)[None, :], (OCTET, full_y))
    constants = [
        *halves(cosine_matrix(extent)),
        *halves(matrix_y.T),
        *halves(matrix_y),
        waves_x.astype(np.float32),
        waves_y.astype(np.float32),
    ]
    slots = ITERS + 1
    real = lambda *shape: pltpu.VMEM(shape, jnp.float32)
    u, b = pl.pallas_call(
        functools.partial(kernel, size_y, size_z),
        out_shape=(
            jax.ShapeDtypeStruct(f.shape, jnp.float32),
            jax.ShapeDtypeStruct(b.shape, jnp.float32),
        ),
        in_specs=[pl.BlockSpec(memory_space=pltpu.VMEM)] * (2 + len(constants)),
        out_specs=(pl.BlockSpec(memory_space=pltpu.VMEM),) * 2,
        scratch_shapes=[
            real(cells_y, cells_z, extent),
            real(octets, extent, LANES),
            real(octets, size_y, part, LANES),
            real(cells_z, part, full_y),
            real(cells_z, part, full_y),
            real(cells_z, part, full_y),
            real(octets, size_y, part, LANES),
            real(octets, extent, LANES),
            real(9, part, full_y),
            real(ITERS, 2, part, full_y),
            real(ITERS, size_z, 2, part, full_y),
            real(size_z, 2, part, full_y),
            real(cells_y, extent),
            real(slots, cells_z, extent),
            real(slots, cells_z, extent),
            real(slots, cells_y, extent),
            real(slots, cells_y, extent),
            real(slots, 2, cells_y, extent),
            real(cells_z, extent),
            real(cells_y, extent),
            pltpu.SemaphoreType.DMA((octets, size_y)),
            pltpu.SemaphoreType.DMA((octets, size_y)),
            pltpu.SemaphoreType.DMA((octets, size_y)),
            pltpu.SemaphoreType.DMA((octets, size_y)),
            pltpu.SemaphoreType.DMA((ITERS, size_z)),
            pltpu.SemaphoreType.DMA((ITERS, size_z)),
            pltpu.SemaphoreType.DMA((slots, 6)),
            pltpu.SemaphoreType.DMA((slots, 6)),
        ],
        compiler_params=pltpu.CompilerParams(collective_id=0, has_side_effects=True),
    )(f, b, *[jnp.asarray(c) for c in constants])
    return jnp.transpose(u, (2, 0, 1)), jnp.transpose(b, (0, 3, 1, 2))


def solution(mesh):
    return jax.shard_map(
        functools.partial(per_device, mesh.shape["gy"], mesh.shape["gz"]),
        mesh=mesh,
        in_specs=(P(None, "gy", "gz"), P(None, None, "gy", "gz")),
        out_specs=(P(None, "gy", "gz"), P(None, None, "gy", "gz")),
        check_vma=False,
    )
```

time: 508 us -> 153 us (0.30); the launches traced: 498 us -> 153 us
  blocking collectives: 238 us -> 0 us
  Pallas kernels: 0 us -> 146 us
  local copies, waits for them, and re-layouts: 69.1 us -> 6.39 us
  matrix products: 57.2 us -> 0 us
  waiting for transfers between devices: 53.4 us -> 0 us
  starting transfers between devices: 43.5 us -> 0 us
  other arithmetic: 34.3 us -> 0 us
    all_to_all x10 -> x0, blocking collectives: 238 us -> none  [the longest x3 87.8 us: solve(): lax.all_to_all(spectra, 'gz', split_axis=2, concat_axis=0, tiled=True)]
    pallas_call x0 -> x1, Pallas kernels: none -> 146 us  [per_device(): pl.pallas_call(functools.partial(kernel, size_y, size_z), out_shape=(jax....]
    all_to_all x2 -> x0, waiting for transfers between devices: 41.7 us -> none  [the longest x1 26.3 us: solve(): lax.all_to_all(spectra, 'gz', split_axis=0, concat_axis=2, tiled=True)]
    unnamed x6 -> x0, matrix products: 35.8 us -> none
    ppermute x14 -> x0, starting transfers between devices: 34.3 us -> none  [shifted(): return lax.ppermute(value, axis, pairs)]
    dot_general x12 -> x0, matrix products: 21.4 us -> none  [transform(): jnp.einsum(patterns[position], matrix, volume, precision=lax.Precision.HI...]
    unnamed x22 -> x2, local copies, waits for them, and re-layouts: 26.4 us -> 6.39 us
    all_to_all x19 -> x0, local copies, waits for them, and re-layouts: 18.7 us -> none  [the longest x10 16.1 us: solve(): lax.all_to_all(spectra, 'gz', split_axis=0, concat_axis=2, tiled=True)]
  transfers between devices with their start and end apart: 16 -> 0, of which waited for: 8 -> 0; matrix products, arithmetic and copies ran while one was open for 1% -> 0% of each run, Pallas kernels for 0% -> 0%
where the time goes in v1:
time: 153 us
  Pallas kernels  146 us (95%)
  local copies, waits for them, and re-layouts  6.39 us (4%)
    pallas_call x1, Pallas kernels, per_device(): pl.pallas_call(functools.partial(kernel, size_y, size_z), out_shape=(jax....  146 us
    unnamed x2, local copies, waits for them, and re-layouts  6.39 us

profile of v1, /device:TPU:0, one launch (start us, length us, event | category | flops | bytes accessed | tf_op | source)
XLA Modules:
  0.0 152.9 jit_solution(2966622975380347921)
XLA Ops:
  0.6 145.9 %shard_map.113 = (f32[16,32,512]{2,1,0:T(8,128)}, f32[3,16,32,512]{3,2,1,0:T(8,128)}) custom-call(f32[16,32,512]{2,1,0:T(8,128)} %bitcast.6, f32[3,16,32,512]{3,2,1,0:T(8,128)} %bitcast.4, bf16[512,512]{1,0:T(8,128)(2,1)} %constant.16.clone.xh, bf16[512,512]{1,0:T(8,128)(2,1)} %constant.17.clone.xl, bf16[128,128]{1,0:T(8,128)(2,1)} %constant.18.clone.yh, ...), custom_call_target="tpu_custom_call" | custom-call | tf_op jit(solution)/shard_map/pallas_call | solution.py:383
  146.6 2.3 %copy.14 = f32[512,16,32]{0,2,1:T(8,128)} copy(f32[512,16,32]{0,2,1:T(8,128)} %bitcast.7) | data formatting | bytes 2097152
  148.9 4.1 %copy.15 = f32[3,512,16,32]{1,3,2,0:T(8,128)} copy(f32[3,512,16,32]{1,3,2,0:T(8,128)} %bitcast.5) | data formatting | bytes 6291456

commit v2 on v1

v2 whole, which is shorter than its diff:
```python
import functools

import jax
import jax.numpy as jnp
import numpy as np
from jax import lax
from jax.experimental import pallas as pl
from jax.experimental.pallas import tpu as pltpu
from jax.sharding import PartitionSpec as P

ITERS = 3
fidelity = 1.0
penalty = 2.0
threshold = 0.5
LANES = 128
OCTET = 8
HALVES = 2


def cosine_matrix(length):
    wave = np.arange(length)[:, None]
    sample = np.arange(length)[None, :]
    factor = np.where(wave == 0, np.sqrt(1.0 / length), np.sqrt(2.0 / length))
    return factor * np.cos(np.pi * ((2 * sample + 1) * wave % (4 * length)) / (2.0 * length))


def laplace_values(length):
    return 4.0 * np.sin(np.pi * np.arange(length) / (2.0 * length)) ** 2


def halves(matrix):
    matrix = matrix.astype(np.float32)
    high = matrix.astype(jnp.bfloat16)
    low = (matrix - high.astype(np.float32)).astype(jnp.bfloat16)
    return high, low


def split(values):
    high = values.astype(jnp.bfloat16)
    return high, (values - high.astype(jnp.float32)).astype(jnp.bfloat16)


def product(left, right, dims):
    dot = functools.partial(
        lax.dot_general, dimension_numbers=(dims, ((), ())), preferred_element_type=jnp.float32
    )
    return dot(left[0], right[0]) + (dot(left[0], right[1]) + dot(left[1], right[0]))


def swap_groups(arrays):
    arrays = list(arrays)
    lane = lax.broadcasted_iota(jnp.int32, arrays[0].shape, 1)
    for bit in (1, 2, 4):
        upper = (lane & bit) != 0
        for low in range(OCTET):
            if low & bit:
                continue
            first, second = arrays[low], arrays[low | bit]
            arrays[low] = jnp.where(upper, pltpu.roll(second, bit, 1), first)
            arrays[low | bit] = jnp.where(upper, second, pltpu.roll(first, LANES - bit, 1))
    return arrays


def clip(values):
    return jnp.minimum(jnp.maximum(values, -threshold), threshold)


def kernel(
    size_y, size_z,
    f_ref, b_in, xh, xl, yh, yl, th, tl, ex_ref, ey_ref,
    u_ref, b_ref,
    src, spec, front, depth, gain, tail, back, arrive, home, ends, gathered, chain, edge,
    next_y, last_y, next_z, last_z, pack_z, low_by, low_bz,
    fs, fr, bs, br, zs, zr, hs, hr, es, er,
):
    iy, iz = lax.axis_index("gy"), lax.axis_index("gz")
    cells_y, cells_z, extent = f_ref.shape
    octets = cells_z // OCTET
    part = extent // size_y
    piece = part // HALVES
    half = extent // HALVES
    groups = size_y // OCTET
    rows = cells_y * OCTET
    full_y = cells_y * size_y
    others_y = range(1, size_y)
    others_z = range(1, size_z)

    def at_y(d):
        return lax.rem(iy + d, size_y)

    def at_z(d):
        return lax.rem(iz + d, size_z)

    def octet(o):
        return pl.ds(o * OCTET, OCTET)

    barrier = pltpu.get_barrier_semaphore()
    for d in others_y:
        pl.semaphore_signal(barrier, inc=1, device_id={"gy": at_y(d)}, device_id_type=pl.DeviceIdType.MESH)
    for d in others_z:
        pl.semaphore_signal(barrier, inc=1, device_id={"gz": at_z(d)}, device_id_type=pl.DeviceIdType.MESH)
    pl.semaphore_wait(barrier, size_y + size_z - 2)

    def remote(source, target, send, recv, device):
        return pltpu.make_async_remote_copy(
            src_ref=source, dst_ref=target, send_sem=send, recv_sem=recv,
            device_id=device, device_id_type=pl.DeviceIdType.MESH,
        )

    def band(h, owner):
        return pl.ds(pl.multiple_of(h * half + owner * piece, piece), piece)

    def inner(h):
        return pl.ds(h * piece, piece)

    def forth(h, o, d):
        return remote(
            spec.at[o, band(h, at_y(d))], front.at[o, iy, inner(h)],
            fs.at[h, o, d], fr.at[h, o, d], {"gy": at_y(d)},
        )

    def home_copy(h, o, d):
        return remote(
            back.at[h, o, at_y(d)], arrive.at[o, band(h, iy)],
            bs.at[h, o, d], br.at[h, o, d], {"gy": at_y(d)},
        )

    def around(slot, h, d):
        return remote(
            ends.at[slot, h], gathered.at[slot, iz, h],
            zs.at[slot, h, d], zr.at[slot, h, d], {"gz": at_z(d)},
        )

    def halo_y(volume, slot, o):
        return [
            remote(
                volume.at[0, octet(o)], next_y.at[slot, octet(o)],
                hs.at[slot, 0, o], hr.at[slot, 0, o], {"gy": at_y(size_y - 1)},
            ),
            remote(
                volume.at[cells_y - 1, octet(o)], last_y.at[slot, octet(o)],
                hs.at[slot, 1, o], hr.at[slot, 1, o], {"gy": at_y(1)},
            ),
        ]

    def halo_next_z(slot):
        return remote(
            pack_z.at[slot, 0], next_z.at[slot], es.at[slot, 0], er.at[slot, 0],
            {"gz": at_z(size_z - 1)},
        )

    def halo_last_z(slot):
        return remote(
            pack_z.at[slot, 1], last_z.at[slot], es.at[slot, 1], er.at[slot, 1], {"gz": at_z(1)}
        )

    def halo_start(volume, slot, o):
        if o == 0:
            pack_z[slot, 0] = volume[:, 0, :]
            halo_next_z(slot).start()
        if o == octets - 1:
            pack_z[slot, 1] = volume[:, cells_z - 1, :]
            halo_last_z(slot).start()
        for copy in halo_y(volume, slot, o):
            copy.start()

    edge[...] = b_in[2, :, cells_z - 1, :]
    extra = [
        remote(b_in.at[1, cells_y - 1], low_by, es.at[0, 2], er.at[0, 2], {"gy": at_y(1)}),
        remote(edge, low_bz, es.at[0, 3], er.at[0, 3], {"gz": at_z(1)}),
    ]
    for copy in extra:
        copy.start()
    for o in range(octets):
        halo_start(f_ref, 0, o)

    waves = jnp.concatenate([ex_ref[band(h, iy), :] for h in range(HALVES)], axis=0)
    centre = fidelity / penalty + 2.0 + jnp.concatenate([waves] * groups, axis=1) + ey_ref[0:1, :]

    def eliminate(first, final, keep):
        level = 1.0 / (centre - first)
        run = level
        corner = level
        if keep:
            gain[0] = level
            tail[0] = run

        def step(j, carry):
            level, run, corner = carry
            level = 1.0 / (centre - jnp.where(j == cells_z - 1, final, 0.0) - level)
            after = run * level
            corner = corner + run * after
            if keep:
                gain[j] = level
                tail[j] = after
            return level, after, corner

        return lax.fori_loop(1, cells_z, step, (level, run, corner))

    def coefficients():
        own_end, own_far, own_start = eliminate(
            jnp.where(iz == 0, 1.0, 0.0), jnp.where(iz == size_z - 1, 1.0, 0.0), True
        )
        mid_end, mid_far, mid_start = eliminate(0.0, 0.0, False)
        linked, _, _ = eliminate(1.0, 0.0, False)
        left_link = jnp.zeros_like(centre)
        right_link = jnp.zeros_like(centre)
        for q in range(size_z - 1):
            if q > 0:
                ratio = mid_far * linked / (1.0 - mid_start * linked)
                chain[q, 0] = mid_far + ratio * mid_start
                chain[q, 1] = ratio
                linked = mid_end + mid_far * ratio
            left_link = jnp.where(iz == q + 1, linked, left_link)
            right_link = jnp.where(size_z - 2 - iz == q, linked, right_link)
        one_l = 1.0 - own_start * left_link
        one_r = 1.0 - own_end * right_link
        cross_l = own_far * left_link
        cross_r = own_far * right_link
        scale = 1.0 / (one_l * one_r - cross_l * cross_r)
        home[0] = left_link
        home[1] = right_link
        home[2] = one_l * scale
        home[3] = one_r * scale
        home[4] = cross_l * scale
        home[5] = cross_r * scale
        home[6] = own_start
        home[7] = own_end
        home[8] = own_far

    row = lax.broadcasted_iota(jnp.int32, (OCTET, extent), 0)
    keep_x = lax.broadcasted_iota(jnp.int32, (OCTET, extent), 1) < extent - 1

    def pointwise(volume, old, slot, first, o):
        at = octet(o)
        final = o == octets - 1

        def flux(slope, was):
            total = slope + was
            new = clip(total)
            return new, total - new - (was if first else new)

        if o == 0:
            if first:
                for copy in extra:
                    copy.wait()
            halo_last_z(slot).wait()
            new, lower_z = flux(pack_z[slot, 0] - last_z[slot], low_bz[...])
            if not first:
                low_bz[...] = new
            edge[...] = jnp.where(iz > 0, lower_z, 0.0)
        if final:
            halo_next_z(slot).wait()

        def plane(y, above, before, keep_y):
            value = volume[y, at, :]
            new, flux_x = flux(
                jnp.where(keep_x, pltpu.roll(value, extent - 1, 1) - value, 0.0), old[0, y, at, :]
            )
            b_ref[0, y, at, :] = old[0, y, at, :] if first else new
            flux_x = jnp.where(keep_x, flux_x, 0.0)
            new, flux_y = flux(jnp.where(keep_y, above - value, 0.0), old[1, y, at, :])
            b_ref[1, y, at, :] = old[1, y, at, :] if first else new
            flux_y = jnp.where(keep_y, flux_y, 0.0)
            if final:
                beyond = next_z[slot, pl.ds(y, 1), :]
                keep_z = jnp.logical_or(row < OCTET - 1, iz < size_z - 1)
            else:
                beyond = volume[y, pl.ds((o + 1) * OCTET, 1), :]
                keep_z = row < OCTET
            beside = jnp.where(row < OCTET - 1, pltpu.roll(value, OCTET - 1, 0), beyond)
            new, flux_z = flux(jnp.where(keep_z, beside - value, 0.0), old[2, y, at, :])
            b_ref[2, y, at, :] = old[2, y, at, :] if first else new
            flux_z = jnp.where(keep_z, flux_z, 0.0)
            under = pltpu.roll(flux_z, 1, 0)
            src[o, y] = (
                (fidelity / penalty) * f_ref[y, at, :]
                + (pltpu.roll(flux_x, 1, 1) - flux_x)
                + (before - flux_y)
                + (jnp.where(row > 0, under, edge[pl.ds(y, 1), :]) - flux_z)
            )
            edge[pl.ds(y, 1), :] = under[0:1, :]
            return flux_y

        _, bottom = flux(volume[1, at, :] - volume[0, at, :], old[1, 0, at, :])
        before = lax.fori_loop(
            1, cells_y - 1, lambda y, before: plane(y, volume[y + 1, at, :], before, True), bottom
        )
        for copy in halo_y(volume, slot, o):
            copy.wait()
        new, lower_y = flux(volume[0, at, :] - last_y[slot, at, :], low_by[at, :])
        if not first:
            low_by[at, :] = new
        plane(0, volume[1, at, :], jnp.where(iy > 0, lower_y, 0.0), True)
        plane(cells_y - 1, next_y[slot, at, :], before, iy < size_y - 1)

    def send_octet(o):
        block = split(src[o].reshape(rows, extent))
        spec[o] = product((xh[...], xl[...]), block, ((1,), (1,)))
        for d in others_y:
            forth(0, o, d).start()
        for h in range(HALVES):
            front[o, iy, inner(h), :] = spec[o, band(h, iy), :]

    def send_rest():
        for h in range(1, HALVES):
            for o in range(octets):
                for d in others_y:
                    forth(h, o, d).start()

    def forward(slot, h):
        level = jnp.zeros((piece, full_y), jnp.float32)
        first = level
        for o in range(octets):
            for d in others_y:
                forth(h, o, d).wait_recv()
            for r in range(piece // OCTET):
                at = pl.ds(h * piece + r * OCTET, OCTET)
                for t in range(groups):
                    planes = swap_groups([front[o, t * OCTET + i, at, :] for i in range(OCTET)])
                    for i in range(OCTET):
                        depth[h, o * OCTET + i, pl.ds(r * OCTET, OCTET), pl.ds(t * LANES, LANES)] = planes[i]
            values = split(depth[h, octet(o)].reshape(OCTET * piece, full_y))
            values = product(values, (yh[...], yl[...]), ((1,), (0,)))
            values = values.reshape(OCTET, piece, full_y)
            for i in range(OCTET):
                j = o * OCTET + i
                level = (values[i] + level) * gain[j, inner(h), :]
                first = level if j == 0 else first + tail[j - 1, inner(h), :] * level
                depth[h, j] = level
        ends[slot, h, 0] = first
        ends[slot, h, 1] = level
        gathered[slot, iz, h, 0] = first
        gathered[slot, iz, h, 1] = level
        for d in others_z:
            around(slot, h, d).start()

    def backward(slot, h):
        for d in others_z:
            around(slot, h, d).wait_recv()
        left = jnp.zeros((piece, full_y), jnp.float32)
        right = left
        for q in range(size_z - 1):
            mirror = size_z - 1 - q
            here = gathered[slot, q, h, 1]
            there = gathered[slot, mirror, h, 0]
            if q > 0:
                near, far = chain[q, 0, inner(h), :], chain[q, 1, inner(h), :]
                here = here + near * left + far * gathered[slot, q, h, 0]
                there = there + near * right + far * gathered[slot, mirror, h, 1]
            left = jnp.where(q < iz, here, left)
            right = jnp.where(q < size_z - 1 - iz, there, right)
        link = [home[i, inner(h), :] for i in range(9)]
        bottom = ends[slot, h, 0] + link[6] * left + link[8] * right
        top = ends[slot, h, 1] + link[8] * left + link[7] * right
        from_left = left + link[0] * (link[3] * bottom + link[5] * top)
        value = right + link[1] * (link[2] * top + link[4] * bottom)
        for o in reversed(range(octets)):
            for i in reversed(range(OCTET)):
                j = o * OCTET + i
                value = (
                    depth[h, j] + from_left * tail[j, inner(h), :] + gain[j, inner(h), :] * value
                )
                depth[h, j] = value
            values = split(depth[h, octet(o)].reshape(OCTET * piece, full_y))
            values = product(values, (th[...], tl[...]), ((1,), (0,)))
            depth[h, octet(o)] = values.reshape(OCTET, piece, full_y)
            for r in range(piece // OCTET):
                at = pl.ds(r * OCTET, OCTET)
                for t in range(groups):
                    planes = swap_groups(
                        [depth[h, o * OCTET + i, at, pl.ds(t * LANES, LANES)] for i in range(OCTET)]
                    )
                    for i in range(OCTET):
                        back[h, o, t * OCTET + i, at, :] = planes[i]
            for d in others_y:
                home_copy(h, o, d).start()
            arrive[o, band(h, iy), :] = back[h, o, iy]

    def assemble(slot, h):
        at = pl.ds(h * half, half)
        for o in reversed(range(octets)):
            for d in others_y:
                home_copy(h, o, d).wait_recv()
            values = product(split(arrive[o, at, :].T), (xh[at, :], xl[at, :]), ((1,), (0,)))
            values = values.reshape(cells_y, OCTET, extent)
            if h > 0:
                values = values + u_ref[:, octet(o), :]
            u_ref[:, octet(o), :] = values
            if h == HALVES - 1:
                halo_start(u_ref, slot + 1, o)

    coefficients()
    for o in range(octets):
        pointwise(f_ref, b_in, 0, True, o)
        send_octet(o)
    send_rest()

    def iteration(slot, carry):
        for h in range(HALVES):
            forward(slot, h)
        for h in range(HALVES):
            backward(slot, h)
        for h in range(HALVES):
            for o in range(octets):
                for d in others_y:
                    forth(h, o, d).wait_send()
        for h in range(HALVES):
            assemble(slot, h)
        for h in range(HALVES):
            for o in range(octets):
                for d in others_y:
                    home_copy(h, o, d).wait_send()
            for d in others_z:
                around(slot, h, d).wait_send()
        for o in range(octets):
            pointwise(u_ref, b_ref, slot + 1, False, o)

            @pl.when(slot < ITERS - 1)
            def _():
                send_octet(o)

        @pl.when(slot < ITERS - 1)
        def _():
            send_rest()

        return carry

    lax.fori_loop(0, ITERS, iteration, 0)


def per_device(size_y, size_z, observed, bregman):
    f = jnp.transpose(observed, (1, 2, 0))
    b = jnp.transpose(bregman, (0, 2, 3, 1))
    cells_y, cells_z, extent = f.shape
    full_y = cells_y * size_y
    part = extent // size_y
    octets = cells_z // OCTET
    groups = size_y // OCTET
    order = np.array(
        [
            (t * OCTET + i) * cells_y + y
            for t in range(groups)
            for y in range(cells_y)
            for i in range(OCTET)
        ]
    )
    matrix_y = cosine_matrix(full_y)[:, order]
    waves_x = np.broadcast_to(laplace_values(extent)[:, None], (extent, LANES))
    waves_y = np.broadcast_to(laplace_values(full_y)[None, :], (OCTET, full_y))
    constants = [
        *halves(cosine_matrix(extent)),
        *halves(matrix_y.T),
        *halves(matrix_y),
        waves_x.astype(np.float32),
        waves_y.astype(np.float32),
    ]
    slots = ITERS + 1
    piece = part // HALVES
    flags = pltpu.SemaphoreType.DMA
    real = lambda *shape: pltpu.VMEM(shape, jnp.float32)
    u, b = pl.pallas_call(
        functools.partial(kernel, size_y, size_z),
        out_shape=(
            jax.ShapeDtypeStruct(f.shape, jnp.float32),
            jax.ShapeDtypeStruct(b.shape, jnp.float32),
        ),
        in_specs=[pl.BlockSpec(memory_space=pltpu.VMEM)] * (2 + len(constants)),
        out_specs=(pl.BlockSpec(memory_space=pltpu.VMEM),) * 2,
        scratch_shapes=[
            real(octets, cells_y, OCTET, extent),
            real(octets, extent, LANES),
            real(octets, size_y, part, LANES),
            real(HALVES, cells_z, piece, full_y),
            real(cells_z, part, full_y),
            real(cells_z, part, full_y),
            real(HALVES, octets, size_y, piece, LANES),
            real(octets, extent, LANES),
            real(9, part, full_y),
            real(ITERS, HALVES, 2, piece, full_y),
            real(ITERS, size_z, HALVES, 2, piece, full_y),
            real(size_z, 2, part, full_y),
            real(cells_y, extent),
            real(slots, cells_z, extent),
            real(slots, cells_z, extent),
            real(slots, cells_y, extent),
            real(slots, cells_y, extent),
            real(slots, 2, cells_y, extent),
            real(cells_z, extent),
            real(cells_y, extent),
            flags((HALVES, octets, size_y)),
            flags((HALVES, octets, size_y)),
            flags((HALVES, octets, size_y)),
            flags((HALVES, octets, size_y)),
            flags((ITERS, HALVES, size_z)),
            flags((ITERS, HALVES, size_z)),
            flags((slots, 2, octets)),
            flags((slots, 2, octets)),
            flags((slots, 4)),
            flags((slots, 4)),
        ],
        compiler_params=pltpu.CompilerParams(collective_id=0, has_side_effects=True),
    )(f, b, *[jnp.asarray(c) for c in constants])
    return jnp.transpose(u, (2, 0, 1)), jnp.transpose(b, (0, 3, 1, 2))


def solution(mesh):
    return jax.shard_map(
        functools.partial(per_device, mesh.shape["gy"], mesh.shape["gz"]),
        mesh=mesh,
        in_specs=(P(None, "gy", "gz"), P(None, None, "gy", "gz")),
        out_specs=(P(None, "gy", "gz"), P(None, None, "gy", "gz")),
        check_vma=False,
    )
```

time: 153 us -> 144 us (0.941)
  Pallas kernels: 146 us -> 137 us
    pallas_call x1, Pallas kernels: 146 us -> 137 us  [per_device(): pl.pallas_call(functools.partial(kernel, size_y, size_z), out_shape=(jax....]
where the time goes in v2:
time: 144 us
  Pallas kernels  137 us (95%)
  local copies, waits for them, and re-layouts  6.39 us (4%)
    pallas_call x1, Pallas kernels, per_device(): pl.pallas_call(functools.partial(kernel, size_y, size_z), out_shape=(jax....  137 us
    unnamed x2, local copies, waits for them, and re-layouts  6.39 us

profile of v2, /device:TPU:0, one launch (start us, length us, event | category | flops | bytes accessed | tf_op | source)
XLA Modules:
  0.0 143.7 jit_solution(17740814172257469297)
XLA Ops:
  0.6 136.7 %shard_map.113 = (f32[16,32,512]{2,1,0:T(8,128)}, f32[3,16,32,512]{3,2,1,0:T(8,128)}) custom-call(f32[16,32,512]{2,1,0:T(8,128)} %bitcast.6, f32[3,16,32,512]{3,2,1,0:T(8,128)} %bitcast.4, bf16[512,512]{1,0:T(8,128)(2,1)} %constant.16.clone.xh, bf16[512,512]{1,0:T(8,128)(2,1)} %constant.17.clone.xl, bf16[128,128]{1,0:T(8,128)(2,1)} %constant.18.clone.yh, ...), custom_call_target="tpu_custom_call" | custom-call | tf_op jit(solution)/shard_map/pallas_call | solution.py:462
  137.3 2.3 %copy.14 = f32[512,16,32]{0,2,1:T(8,128)} copy(f32[512,16,32]{0,2,1:T(8,128)} %bitcast.7) | data formatting | bytes 2097152
  139.6 4.1 %copy.15 = f32[3,512,16,32]{1,3,2,0:T(8,128)} copy(f32[3,512,16,32]{1,3,2,0:T(8,128)} %bitcast.5) | data formatting | bytes 6291456

commit v3 on v2

--- a/solution.py
+++ b/solution.py
@@ -69,7 +69,7 @@
     size_y, size_z,
     f_ref, b_in, xh, xl, yh, yl, th, tl, ex_ref, ey_ref,
     u_ref, b_ref,
-    src, spec, front, depth, gain, tail, back, arrive, home, ends, gathered, chain, edge,
+    src, spec, front, depth, gain, tail, back, arrive, home, ends, gathered, chain, edge, border,
     next_y, last_y, next_z, last_z, pack_z, low_by, low_bz,
     fs, fr, bs, br, zs, zr, hs, hr, es, er,
 ):
@@ -248,7 +248,9 @@
             new, lower_z = flux(pack_z[slot, 0] - last_z[slot], low_bz[...])
             if not first:
                 low_bz[...] = new
-            edge[...] = jnp.where(iz > 0, lower_z, 0.0)
+            lower_z = jnp.where(iz > 0, lower_z, 0.0)
+            for y in range(cells_y):
+                border[y, 0:1, :] = lower_z[y : y + 1, :]
         if final:
             halo_next_z(slot).wait()
 
@@ -277,15 +279,22 @@
                 (fidelity / penalty) * f_ref[y, at, :]
                 + (pltpu.roll(flux_x, 1, 1) - flux_x)
                 + (before - flux_y)
-                + (jnp.where(row > 0, under, edge[pl.ds(y, 1), :]) - flux_z)
+                + (jnp.where(row > 0, under, border[y]) - flux_z)
             )
-            edge[pl.ds(y, 1), :] = under[0:1, :]
+            border[y] = under
             return flux_y
 
         _, bottom = flux(volume[1, at, :] - volume[0, at, :], old[1, 0, at, :])
-        before = lax.fori_loop(
-            1, cells_y - 1, lambda y, before: plane(y, volume[y + 1, at, :], before, True), bottom
-        )
+        inside = cells_y - 2
+        steps = max(u for u in range(1, 8) if inside % u == 0)
+
+        def several(k, before):
+            for i in range(steps):
+                y = 1 + k * steps + i
+                before = plane(y, volume[y + 1, at, :], before, True)
+            return before
+
+        before = lax.fori_loop(0, inside // steps, several, bottom)
         for copy in halo_y(volume, slot, o):
             copy.wait()
         new, lower_y = flux(volume[0, at, :] - last_y[slot, at, :], low_by[at, :])
@@ -481,6 +490,7 @@
             real(ITERS, size_z, HALVES, 2, piece, full_y),
             real(size_z, 2, part, full_y),
             real(cells_y, extent),
+            real(cells_y, OCTET, extent),
             real(slots, cells_z, extent),
             real(slots, cells_z, extent),
             real(slots, cells_y, extent),

time: 144 us -> 124 us (0.86)
  Pallas kernels: 137 us -> 116 us
    pallas_call x1, Pallas kernels: 137 us -> 116 us  [per_device(): pl.pallas_call(functools.partial(kernel, size_y, size_z), out_shape=(jax....]
where the time goes in v3:
time: 124 us; the launch traced here: 123 us
  Pallas kernels  116 us (94%)
  local copies, waits for them, and re-layouts  6.39 us (5%)
    pallas_call x1, Pallas kernels, per_device(): pl.pallas_call(functools.partial(kernel, size_y, size_z), out_shape=(jax....  116 us
    unnamed x2, local copies, waits for them, and re-layouts  6.39 us

profile of v3, /device:TPU:0, one launch (start us, length us, event | category | flops | bytes accessed | tf_op | source)
XLA Modules:
  0.0 123.3 jit_solution(899426659582886302)
XLA Ops:
  0.6 116.3 %shard_map.113 = (f32[16,32,512]{2,1,0:T(8,128)}, f32[3,16,32,512]{3,2,1,0:T(8,128)}) custom-call(f32[16,32,512]{2,1,0:T(8,128)} %bitcast.6, f32[3,16,32,512]{3,2,1,0:T(8,128)} %bitcast.4, bf16[512,512]{1,0:T(8,128)(2,1)} %constant.16.clone.xh, bf16[512,512]{1,0:T(8,128)(2,1)} %constant.17.clone.xl, bf16[128,128]{1,0:T(8,128)(2,1)} %constant.18.clone.yh, ...), custom_call_target="tpu_custom_call" | custom-call | tf_op jit(solution)/shard_map/pallas_call | solution.py:471
  116.9 2.3 %copy.14 = f32[512,16,32]{0,2,1:T(8,128)} copy(f32[512,16,32]{0,2,1:T(8,128)} %bitcast.7) | data formatting | bytes 2097152
  119.2 4.1 %copy.15 = f32[3,512,16,32]{1,3,2,0:T(8,128)} copy(f32[3,512,16,32]{1,3,2,0:T(8,128)} %bitcast.5) | data formatting | bytes 6291456
